TPU v7x, 32 devices: a whole 2x2x4 slice. The times are simulated.
32 devices in a mesh: models: 1, leaf: 32 (over z, y, x, core).
Axes of the slice: x: 2, y: 2, z: 4, core: 2. Of those that a mesh axis runs over, the one named last changes fastest.
Arguments:
- slip_rate: float32 [131072], P(('models', 'leaf')), may hold values from -6 to 6
- near_blocks: bfloat16 [512, 3, 256, 256], P(('models', 'leaf')), may hold values from -0.21875 to 0.21875
- near_index: int32 [512, 3], P(('models', 'leaf')), may hold values from 0 to 511, as said below
- far_left: bfloat16 [9, 32, 131072], P(None, None, ('models', 'leaf')), may hold values from -1 to 1
- far_right: bfloat16 [9, 32, 131072], P(None, None, ('models', 'leaf')), may hold values from -6 to 6
- far_ranks: int32 [512, 9], P(('models', 'leaf')), may hold values from 8 to 32
Outputs:
- first_stress: float32 [131072], P(('models', 'leaf'))
- second_stress: float32 [131072], P(('models', 'leaf'))
Inputs may be any that keep to these rules, and one draw needn't show every extreme that they name: near_index[i, 0] = i; every other entry is a leaf j != i with |j - i| <= 16, and distance 16 occurs.
All inputs are finite; a program needn't handle non-finite values.
Results may differ from a plain program's by a relative error of at most 0.0045.
Values may be sent and summed in bfloat16 or wider, within the bound.
A program may use at most 64 MiB of HBM per device.

v0:
```python
import math

import jax
import jax.numpy as jnp
from jax import lax
from jax.sharding import PartitionSpec as P


def partner_2(value, axis, stride):
    return lax.ppermute(value, axis, [(i, i ^ 1 << stride) for i in range(lax.axis_size(axis))])


def padded(block, sides, width):
    for axis, dim in sides:
        count = lax.axis_size(axis)
        forward = [(i, i + 1) for i in range(count - 1)]
        backward = [(target, source) for source, target in forward]
        low = lax.ppermute(
            lax.slice_in_dim(block, block.shape[dim] - width, None, axis=dim), axis, forward
        )
        high = lax.ppermute(lax.slice_in_dim(block, 0, width, axis=dim), axis, backward)
        block = jnp.concatenate([low, block, high], axis=dim)
    return block


def far_partners(device_sums, cross_levels):
    outputs = []
    accumulated = device_sums
    for bit_no in range(cross_levels):
        received = partner_2(accumulated, "leaf", bit_no)
        outputs.append(received[bit_no])
        accumulated = accumulated + received
    return outputs


def matvec(operand, near_blocks, near_index, far_left, far_right, far_ranks):
    local_leaves = near_blocks.shape[0]
    leaf_size = near_blocks.shape[2]
    levels = far_left.shape[0]
    rank_cols = far_left.shape[1]
    slip_rows = operand.reshape(local_leaves, leaf_size)
    extended = padded(slip_rows, (("leaf", 0),), local_leaves)
    offset = lax.axis_index("leaf") * local_leaves - local_leaves
    position = near_index - offset
    onehot = (
        position[:, :, None] == jnp.arange(3 * local_leaves, dtype=jnp.int32)[None, None, :]
    ).astype(jnp.bfloat16)
    picked = jnp.einsum("ikj,jp->ikp", onehot, extended, preferred_element_type=jnp.float32).astype(
        jnp.bfloat16
    )
    result = jnp.einsum("ikpq,ikq->ip", near_blocks, picked, preferred_element_type=jnp.float32)
    right_part = far_right.reshape(levels, rank_cols, local_leaves, leaf_size)
    projected = jnp.einsum(
        "lrcp,cp->lcr", right_part, slip_rows, preferred_element_type=jnp.float32
    )
    local_levels = local_leaves.bit_length() - 1
    cross_levels = levels - local_levels
    columns = []
    for level_no in range(local_levels):
        span_size = 2**level_no
        cluster_sums = (
            projected[level_no].reshape(local_leaves // span_size, span_size, rank_cols).sum(axis=1)
        )
        cluster_sums = cluster_sums * (1.0 / math.sqrt(leaf_size * span_size))
        partner = cluster_sums.reshape(-1, 2, rank_cols)[:, ::-1, :].reshape(-1, rank_cols)
        columns.append(jnp.repeat(partner, span_size, axis=0))
    device_sums = jnp.sum(projected[local_levels:], axis=1)
    partner_list = far_partners(device_sums, cross_levels)
    for bit_no in range(cross_levels):
        scale = 1.0 / math.sqrt(leaf_size * 2 ** (local_levels + bit_no))
        columns.append(
            jnp.broadcast_to(partner_list[bit_no][None, :] * scale, (local_leaves, rank_cols))
        )
    stacked = jnp.stack(columns)
    rank_mask = (
        jnp.arange(rank_cols, dtype=jnp.int32)[None, None, :] < jnp.transpose(far_ranks)[:, :, None]
    )
    weights = jnp.where(rank_mask, stacked, 0.0).astype(jnp.bfloat16)
    left_part = far_left.reshape(levels, rank_cols, local_leaves, leaf_size)
    result = result + jnp.einsum(
        "lrcp,lcr->cp", left_part, weights, preferred_element_type=jnp.float32
    )
    return result.reshape(-1)


def local(slip_rate, near_blocks, near_index, far_left, far_right, far_ranks):
    slip_bf = slip_rate.astype(jnp.bfloat16)
    first_stress = matvec(slip_bf, near_blocks, near_index, far_left, far_right, far_ranks)
    relaxed = slip_rate + jnp.tanh(first_stress / 3.0)
    relaxed_bf = relaxed.astype(jnp.bfloat16)
    second_stress = matvec(relaxed_bf, near_blocks, near_index, far_left, far_right, far_ranks)
    return (first_stress, second_stress)


def solution(mesh):
    in_specs = (
        P(("models", "leaf")),
        P(("models", "leaf"), None, None, None),
        P(("models", "leaf"), None),
        P(None, None, ("models", "leaf")),
        P(None, None, ("models", "leaf")),
        P(("models", "leaf"), None),
    )
    out_specs = (P(("models", "leaf")), P(("models", "leaf")))
    return jax.shard_map(local, mesh=mesh, in_specs=in_specs, out_specs=out_specs, check_vma=False)
```

profile of v0, /device:TPU:0, one launch (start us, length us, event | category | flops | bytes accessed | tf_op | source)
XLA Modules:
  0.0 65.9 jit_solution(17152655184907252473)
XLA Ops:
  2.8 3.0 %collective-permute-start = (bf16[16,256]{1,0:T(8,128)(2,1)S(1)}, bf16[16,256]{1,0:T(8,128)(2,1)S(1)}, u32[]{:S(2)}, u32[]{:S(2)}) collective-permute-start(bf16[16,256]{1,0:T(8,128)(2,1)S(1)} %reshape.92), channel_id=1, source_target_pairs={{0,1},{1,2},{2,3},{3,4},{4,5},{5,6},{6,7},{7,8},{8,9},{9,10},{10,1... | collective-permute-start | bytes 24584 | tf_op jit(solution)/shard_map/ppermute | solution.py:18
  5.9 3.2 %fusion.6 = f32[16,1,9,32]{3,1,2,0:T(1,128)S(1)} fusion(bf16[16,256,1,1]{1,2,3,0:T(2,128)(2,1)S(1)} %reshape.117, bf16[9,4,16,8,256]{4,3,2,1,0:T(8,128)(2,1)} %bitcast.125), kind=kOutput, calls=%fused_computation.6 | convolution fusion | flops 2359296 | bytes 2385920 | tf_op jit(solution)/shard_map/lrcp,cp->lcr/dot_general | solution.py:53
  9.1 2.7 %collective-permute-start.2 = (f32[5,32]{1,0:T(8,128)S(1)}, f32[5,32]{1,0:T(8,128)S(1)}, u32[]{:S(2)}, u32[]{:S(2)}) collective-permute-start(f32[5,32]{1,0:T(8,128)S(1)} %slice_reduce_fusion.1), channel_id=1, source_target_pairs={{0,1},{1,0},{2,3},{3,2},{4,5},{5,4},{6,7},{7,6},{8,9},{9,8},{10,11... | collective-permute-start | bytes 1928 | tf_op jit(solution)/shard_map/ppermute | solution.py:10
  12.6 2.4 %collective-permute-start.3 = (f32[5,32]{1,0:T(8,128)S(1)}, f32[5,32]{1,0:T(8,128)S(1)}, u32[]{:S(2)}, u32[]{:S(2)}) collective-permute-start(f32[5,32]{1,0:T(8,128)S(1)} %add.34), channel_id=1, source_target_pairs={{0,2},{1,3},{2,0},{3,1},{4,6},{5,7},{6,4},{7,5},{8,10},{9,11},{10,... | collective-permute-start | bytes 1928 | tf_op jit(solution)/shard_map/ppermute | solution.py:10
  15.0 1.6 %collective-permute-done.3 = f32[5,32]{1,0:T(8,128)S(1)} collective-permute-done((f32[5,32]{1,0:T(8,128)S(1)}, f32[5,32]{1,0:T(8,128)S(1)}, u32[]{:S(2)}, u32[]{:S(2)}) %collective-permute-start.3) | collective-permute-done | bytes 672 | tf_op jit(solution)/shard_map/ppermute | solution.py:10
  16.6 2.4 %collective-permute-start.4 = (f32[5,32]{1,0:T(8,128)S(1)}, f32[5,32]{1,0:T(8,128)S(1)}, u32[]{:S(2)}, u32[]{:S(2)}) collective-permute-start(f32[5,32]{1,0:T(8,128)S(1)} %add.35), channel_id=1, source_target_pairs={{0,4},{1,5},{2,6},{3,7},{4,0},{5,1},{6,2},{7,3},{8,12},{9,13},{10,... | collective-permute-start | bytes 1928 | tf_op jit(solution)/shard_map/ppermute | solution.py:10
  19.0 1.6 %collective-permute-done.4 = f32[5,32]{1,0:T(8,128)S(1)} collective-permute-done((f32[5,32]{1,0:T(8,128)S(1)}, f32[5,32]{1,0:T(8,128)S(1)}, u32[]{:S(2)}, u32[]{:S(2)}) %collective-permute-start.4) | collective-permute-done | bytes 672 | tf_op jit(solution)/shard_map/ppermute | solution.py:10
  20.6 1.6 %collective-permute-start.5 = (f32[5,32]{1,0:T(8,128)S(1)}, f32[5,32]{1,0:T(8,128)S(1)}, u32[]{:S(2)}, u32[]{:S(2)}) collective-permute-start(f32[5,32]{1,0:T(8,128)S(1)} %add.36), channel_id=1, source_target_pairs={{0,8},{1,9},{2,10},{3,11},{4,12},{5,13},{6,14},{7,15},{8,0},{9,1},... | collective-permute-start | bytes 1928 | tf_op jit(solution)/shard_map/ppermute | solution.py:10
  22.2 2.0 %collective-permute-done.5 = f32[5,32]{1,0:T(8,128)S(1)} collective-permute-done((f32[5,32]{1,0:T(8,128)S(1)}, f32[5,32]{1,0:T(8,128)S(1)}, u32[]{:S(2)}, u32[]{:S(2)}) %collective-permute-start.5) | collective-permute-done | bytes 672 | tf_op jit(solution)/shard_map/ppermute | solution.py:10
  24.2 2.6 %collective-permute-start.6 = (f32[5,32]{1,0:T(8,128)S(1)}, f32[5,32]{1,0:T(8,128)S(1)}, u32[]{:S(2)}, u32[]{:S(2)}) collective-permute-start(f32[5,32]{1,0:T(8,128)S(1)} %add.37), channel_id=1, source_target_pairs={{0,16},{1,17},{2,18},{3,19},{4,20},{5,21},{6,22},{7,23},{8,24},{9,... | collective-permute-start | bytes 1928 | tf_op jit(solution)/shard_map/ppermute | solution.py:10
  26.8 1.9 %collective-permute-done.6 = f32[5,32]{1,0:T(8,128)S(1)} collective-permute-done((f32[5,32]{1,0:T(8,128)S(1)}, f32[5,32]{1,0:T(8,128)S(1)}, u32[]{:S(2)}, u32[]{:S(2)}) %collective-permute-start.6) | collective-permute-done | bytes 672 | tf_op jit(solution)/shard_map/ppermute | solution.py:10
  29.5 4.7 %fusion.16 = f32[16,1,256,1]{2,1,3,0:T(1,128)S(1)} fusion(bf16[16,3,256,256]{3,2,1,0:T(8,128)(2,1)} %param.7, bf16[16,3,256,1]{2,1,0,3:T(4,128)(2,1)S(1)} %bitcast.133), kind=kOutput, calls=%fused_computation.23 | convolution fusion | flops 6291456 | bytes 6332416 | tf_op jit(solution)/shard_map/ikpq,ikq->ip/dot_general | solution.py:51
  35.6 3.0 %collective-permute-start.7 = (bf16[16,256]{1,0:T(8,128)(2,1)S(1)}, bf16[16,256]{1,0:T(8,128)(2,1)S(1)}, u32[]{:S(2)}, u32[]{:S(2)}) collective-permute-start(bf16[16,256]{1,0:T(8,128)(2,1)S(1)} %reshape.98), channel_id=1, source_target_pairs={{0,1},{1,2},{2,3},{3,4},{4,5},{5,6},{6,7},{7,8},{8,9},{9,10},{10,1... | collective-permute-start | bytes 24584 | tf_op jit(solution)/shard_map/ppermute | solution.py:18
  38.6 1.5 %fusion.4 = f32[16,1,9,32]{3,1,2,0:T(1,128)S(1)} fusion(bf16[16,256,1,1]{1,2,3,0:T(2,128)(2,1)S(1)} %reshape.119, bf16[9,4,16,8,256]{4,3,2,1,0:T(8,128)(2,1)S(1)} %bitcast.126), kind=kOutput, calls=%fused_computation.4 | convolution fusion | flops 2359296 | bytes 2385920 | tf_op jit(solution)/shard_map/lrcp,cp->lcr/dot_general | solution.py:53
  40.4 1.7 %collective-permute-start.9 = (f32[5,32]{1,0:T(8,128)S(1)}, f32[5,32]{1,0:T(8,128)S(1)}, u32[]{:S(2)}, u32[]{:S(2)}) collective-permute-start(f32[5,32]{1,0:T(8,128)S(1)} %slice_reduce_fusion), channel_id=1, source_target_pairs={{0,1},{1,0},{2,3},{3,2},{4,5},{5,4},{6,7},{7,6},{8,9},{9,8},{10,11... | collective-permute-start | bytes 1928 | tf_op jit(solution)/shard_map/ppermute | solution.py:10
  44.4 2.1 %collective-permute-done.10 = f32[5,32]{1,0:T(8,128)S(1)} collective-permute-done((f32[5,32]{1,0:T(8,128)S(1)}, f32[5,32]{1,0:T(8,128)S(1)}, u32[]{:S(2)}, u32[]{:S(2)}) %collective-permute-start.10) | collective-permute-done | bytes 672 | tf_op jit(solution)/shard_map/ppermute | solution.py:10
  46.5 2.0 %collective-permute-start.11 = (f32[5,32]{1,0:T(8,128)S(1)}, f32[5,32]{1,0:T(8,128)S(1)}, u32[]{:S(2)}, u32[]{:S(2)}) collective-permute-start(f32[5,32]{1,0:T(8,128)S(1)} %add.41), channel_id=1, source_target_pairs={{0,4},{1,5},{2,6},{3,7},{4,0},{5,1},{6,2},{7,3},{8,12},{9,13},{10,... | collective-permute-start | bytes 1928 | tf_op jit(solution)/shard_map/ppermute | solution.py:10
  48.6 1.6 %collective-permute-done.11 = f32[5,32]{1,0:T(8,128)S(1)} collective-permute-done((f32[5,32]{1,0:T(8,128)S(1)}, f32[5,32]{1,0:T(8,128)S(1)}, u32[]{:S(2)}, u32[]{:S(2)}) %collective-permute-start.11) | collective-permute-done | bytes 672 | tf_op jit(solution)/shard_map/ppermute | solution.py:10
  50.2 1.6 %collective-permute-start.12 = (f32[5,32]{1,0:T(8,128)S(1)}, f32[5,32]{1,0:T(8,128)S(1)}, u32[]{:S(2)}, u32[]{:S(2)}) collective-permute-start(f32[5,32]{1,0:T(8,128)S(1)} %add.42), channel_id=1, source_target_pairs={{0,8},{1,9},{2,10},{3,11},{4,12},{5,13},{6,14},{7,15},{8,0},{9,1},... | collective-permute-start | bytes 1928 | tf_op jit(solution)/shard_map/ppermute | solution.py:10
  51.7 2.0 %collective-permute-done.12 = f32[5,32]{1,0:T(8,128)S(1)} collective-permute-done((f32[5,32]{1,0:T(8,128)S(1)}, f32[5,32]{1,0:T(8,128)S(1)}, u32[]{:S(2)}, u32[]{:S(2)}) %collective-permute-start.12) | collective-permute-done | bytes 672 | tf_op jit(solution)/shard_map/ppermute | solution.py:10
  53.8 2.6 %collective-permute-start.13 = (f32[5,32]{1,0:T(8,128)S(1)}, f32[5,32]{1,0:T(8,128)S(1)}, u32[]{:S(2)}, u32[]{:S(2)}) collective-permute-start(f32[5,32]{1,0:T(8,128)S(1)} %add.43), channel_id=1, source_target_pairs={{0,16},{1,17},{2,18},{3,19},{4,20},{5,21},{6,22},{7,23},{8,24},{9,... | collective-permute-start | bytes 1928 | tf_op jit(solution)/shard_map/ppermute | solution.py:10
  56.4 1.9 %collective-permute-done.13 = f32[5,32]{1,0:T(8,128)S(1)} collective-permute-done((f32[5,32]{1,0:T(8,128)S(1)}, f32[5,32]{1,0:T(8,128)S(1)}, u32[]{:S(2)}, u32[]{:S(2)}) %collective-permute-start.13) | collective-permute-done | bytes 672 | tf_op jit(solution)/shard_map/ppermute | solution.py:10
  58.4 2.2 %fusion = f32[16,1,256,1]{2,1,3,0:T(1,128)S(1)} fusion(bf16[9,4,16,8,256]{4,3,2,1,0:T(8,128)(2,1)} %bitcast.159, bf16[9,16,32,1]{2,1,0,3:T(8,128)(2,1)S(1)} %fusion.19), kind=kOutput, calls=%fused_computation | convolution fusion | flops 2359296 | bytes 2384896 | tf_op jit(solution)/shard_map/lrcp,lcr->cp/dot_general | solution.py:80
  60.7 4.5 %fusion.14 = f32[16,1,256,1]{2,1,3,0:T(1,128)S(1)} fusion(bf16[16,3,256,256]{3,2,1,0:T(8,128)(2,1)} %param.7, bf16[16,3,256,1]{2,1,0,3:T(4,128)(2,1)S(1)} %bitcast.134), kind=kOutput, calls=%fused_computation.21 | convolution fusion | flops 6291456 | bytes 6332416 | tf_op jit(solution)/shard_map/ikpq,ikq->ip/dot_general | solution.py:51
  (110 shorter events, 8.7 us)
Async XLA Ops:
  0.6 11.2 %copy-start.4 = (s32[16,3]{0,1:T(4,128)S(1)}, s32[16,3]{0,1:T(4,128)}, u32[]{:S(2)}) copy-start(s32[16,3]{0,1:T(4,128)} %param.8) | copy-start | bytes 580
  0.6 11.6 %copy-start.3 = (s32[16,9]{1,0:T(8,128)S(1)}, s32[16,9]{1,0:T(8,128)}, u32[]{:S(2)}) copy-start(s32[16,9]{1,0:T(8,128)} %param.11) | copy-start | bytes 1732
  0.6 28.1 %copy-start.5 = (bf16[9,32,4096]{2,1,0:T(8,128)(2,1)S(1)}, bf16[9,32,4096]{2,1,0:T(8,128)(2,1)}, u32[]{:S(2)}) copy-start(bf16[9,32,4096]{2,1,0:T(8,128)(2,1)} %param.9) | copy-start | bytes 7077892
  1.5 27.8 %collective-permute-start.1 = (bf16[16,256]{1,0:T(8,128)(2,1)S(1)}, bf16[16,256]{1,0:T(8,128)(2,1)S(1)}, u32[]{:S(2)}, u32[]{:S(2)}) collective-permute-start(bf16[16,256]{1,0:T(8,128)(2,1)S(1)} %reshape.92), channel_id=1, source_target_pairs={{1,0},{2,1},{3,2},{4,3},{5,4},{6,5},{7,6},{8,7},{9,8},{10,9},{11,1... | collective-permute-start | bytes 24584 | tf_op jit(solution)/shard_map/ppermute | solution.py:21
  2.8 26.5 %collective-permute-start = (bf16[16,256]{1,0:T(8,128)(2,1)S(1)}, bf16[16,256]{1,0:T(8,128)(2,1)S(1)}, u32[]{:S(2)}, u32[]{:S(2)}) collective-permute-start(bf16[16,256]{1,0:T(8,128)(2,1)S(1)} %reshape.92), channel_id=1, source_target_pairs={{0,1},{1,2},{2,3},{3,4},{4,5},{5,6},{6,7},{7,8},{8,9},{9,10},{10,1... | collective-permute-start | bytes 24584 | tf_op jit(solution)/shard_map/ppermute | solution.py:18
  9.1 3.5 %collective-permute-start.2 = (f32[5,32]{1,0:T(8,128)S(1)}, f32[5,32]{1,0:T(8,128)S(1)}, u32[]{:S(2)}, u32[]{:S(2)}) collective-permute-start(f32[5,32]{1,0:T(8,128)S(1)} %slice_reduce_fusion.1), channel_id=1, source_target_pairs={{0,1},{1,0},{2,3},{3,2},{4,5},{5,4},{6,7},{7,6},{8,9},{9,8},{10,11... | collective-permute-start | bytes 1928 | tf_op jit(solution)/shard_map/ppermute | solution.py:10
  12.6 3.9 %collective-permute-start.3 = (f32[5,32]{1,0:T(8,128)S(1)}, f32[5,32]{1,0:T(8,128)S(1)}, u32[]{:S(2)}, u32[]{:S(2)}) collective-permute-start(f32[5,32]{1,0:T(8,128)S(1)} %add.34), channel_id=1, source_target_pairs={{0,2},{1,3},{2,0},{3,1},{4,6},{5,7},{6,4},{7,5},{8,10},{9,11},{10,... | collective-permute-start | bytes 1928 | tf_op jit(solution)/shard_map/ppermute | solution.py:10
  16.6 4.0 %collective-permute-start.4 = (f32[5,32]{1,0:T(8,128)S(1)}, f32[5,32]{1,0:T(8,128)S(1)}, u32[]{:S(2)}, u32[]{:S(2)}) collective-permute-start(f32[5,32]{1,0:T(8,128)S(1)} %add.35), channel_id=1, source_target_pairs={{0,4},{1,5},{2,6},{3,7},{4,0},{5,1},{6,2},{7,3},{8,12},{9,13},{10,... | collective-permute-start | bytes 1928 | tf_op jit(solution)/shard_map/ppermute | solution.py:10
  20.6 3.6 %collective-permute-start.5 = (f32[5,32]{1,0:T(8,128)S(1)}, f32[5,32]{1,0:T(8,128)S(1)}, u32[]{:S(2)}, u32[]{:S(2)}) collective-permute-start(f32[5,32]{1,0:T(8,128)S(1)} %add.36), channel_id=1, source_target_pairs={{0,8},{1,9},{2,10},{3,11},{4,12},{5,13},{6,14},{7,15},{8,0},{9,1},... | collective-permute-start | bytes 1928 | tf_op jit(solution)/shard_map/ppermute | solution.py:10
  24.2 4.5 %collective-permute-start.6 = (f32[5,32]{1,0:T(8,128)S(1)}, f32[5,32]{1,0:T(8,128)S(1)}, u32[]{:S(2)}, u32[]{:S(2)}) collective-permute-start(f32[5,32]{1,0:T(8,128)S(1)} %add.37), channel_id=1, source_target_pairs={{0,16},{1,17},{2,18},{3,19},{4,20},{5,21},{6,22},{7,23},{8,24},{9,... | collective-permute-start | bytes 1928 | tf_op jit(solution)/shard_map/ppermute | solution.py:10
  29.5 4.7 %copy-start.1 = (f32[4096]{0:T(1024)S(1)}, f32[4096]{0:T(1024)}, u32[]{:S(2)}) copy-start(f32[4096]{0:T(1024)} %param.6) | copy-start | bytes 49156
  29.5 9.1 %copy-start = (bf16[9,32,4096]{2,1,0:T(8,128)(2,1)S(1)}, bf16[9,32,4096]{2,1,0:T(8,128)(2,1)}, u32[]{:S(2)}) copy-start(bf16[9,32,4096]{2,1,0:T(8,128)(2,1)} %param.10) | copy-start | bytes 7077892
  34.2 26.4 %copy-start.2 = (f32[2,2,8,128]{3,1,2,0:T(2,128)}, f32[2,2,8,128]{3,1,2,0:T(2,128)S(1)}, u32[]{:S(2)}) copy-start(f32[2,2,8,128]{3,1,2,0:T(2,128)S(1)} %copy.35) | copy-start | bytes 49156
  34.3 26.3 %collective-permute-start.8 = (bf16[16,256]{1,0:T(8,128)(2,1)S(1)}, bf16[16,256]{1,0:T(8,128)(2,1)S(1)}, u32[]{:S(2)}, u32[]{:S(2)}) collective-permute-start(bf16[16,256]{1,0:T(8,128)(2,1)S(1)} %reshape.98), channel_id=1, source_target_pairs={{1,0},{2,1},{3,2},{4,3},{5,4},{6,5},{7,6},{8,7},{9,8},{10,9},{11,1... | collective-permute-start | bytes 24584 | tf_op jit(solution)/shard_map/ppermute | solution.py:21
  35.6 25.0 %collective-permute-start.7 = (bf16[16,256]{1,0:T(8,128)(2,1)S(1)}, bf16[16,256]{1,0:T(8,128)(2,1)S(1)}, u32[]{:S(2)}, u32[]{:S(2)}) collective-permute-start(bf16[16,256]{1,0:T(8,128)(2,1)S(1)} %reshape.98), channel_id=1, source_target_pairs={{0,1},{1,2},{2,3},{3,4},{4,5},{5,6},{6,7},{7,8},{8,9},{9,10},{10,1... | collective-permute-start | bytes 24584 | tf_op jit(solution)/shard_map/ppermute | solution.py:18
  40.4 2.5 %collective-permute-start.9 = (f32[5,32]{1,0:T(8,128)S(1)}, f32[5,32]{1,0:T(8,128)S(1)}, u32[]{:S(2)}, u32[]{:S(2)}) collective-permute-start(f32[5,32]{1,0:T(8,128)S(1)} %slice_reduce_fusion), channel_id=1, source_target_pairs={{0,1},{1,0},{2,3},{3,2},{4,5},{5,4},{6,7},{7,6},{8,9},{9,8},{10,11... | collective-permute-start | bytes 1928 | tf_op jit(solution)/shard_map/ppermute | solution.py:10
  42.9 3.6 %collective-permute-start.10 = (f32[5,32]{1,0:T(8,128)S(1)}, f32[5,32]{1,0:T(8,128)S(1)}, u32[]{:S(2)}, u32[]{:S(2)}) collective-permute-start(f32[5,32]{1,0:T(8,128)S(1)} %add.40), channel_id=1, source_target_pairs={{0,2},{1,3},{2,0},{3,1},{4,6},{5,7},{6,4},{7,5},{8,10},{9,11},{10,... | collective-permute-start | bytes 1928 | tf_op jit(solution)/shard_map/ppermute | solution.py:10
  46.5 3.6 %collective-permute-start.11 = (f32[5,32]{1,0:T(8,128)S(1)}, f32[5,32]{1,0:T(8,128)S(1)}, u32[]{:S(2)}, u32[]{:S(2)}) collective-permute-start(f32[5,32]{1,0:T(8,128)S(1)} %add.41), channel_id=1, source_target_pairs={{0,4},{1,5},{2,6},{3,7},{4,0},{5,1},{6,2},{7,3},{8,12},{9,13},{10,... | collective-permute-start | bytes 1928 | tf_op jit(solution)/shard_map/ppermute | solution.py:10
  50.2 3.6 %collective-permute-start.12 = (f32[5,32]{1,0:T(8,128)S(1)}, f32[5,32]{1,0:T(8,128)S(1)}, u32[]{:S(2)}, u32[]{:S(2)}) collective-permute-start(f32[5,32]{1,0:T(8,128)S(1)} %add.42), channel_id=1, source_target_pairs={{0,8},{1,9},{2,10},{3,11},{4,12},{5,13},{6,14},{7,15},{8,0},{9,1},... | collective-permute-start | bytes 1928 | tf_op jit(solution)/shard_map/ppermute | solution.py:10
  53.8 4.5 %collective-permute-start.13 = (f32[5,32]{1,0:T(8,128)S(1)}, f32[5,32]{1,0:T(8,128)S(1)}, u32[]{:S(2)}, u32[]{:S(2)}) collective-permute-start(f32[5,32]{1,0:T(8,128)S(1)} %add.43), channel_id=1, source_target_pairs={{0,16},{1,17},{2,18},{3,19},{4,20},{5,21},{6,22},{7,23},{8,24},{9,... | collective-permute-start | bytes 1928 | tf_op jit(solution)/shard_map/ppermute | solution.py:10
where the time goes:
time: 66.2 us; the launch traced here: 65.9 us
  starting transfers between devices  29.6 us (45%)
  matrix products  16.8 us (25%)
  waiting for transfers between devices  15.6 us (24%)
  other arithmetic  1.44 us (2%)
  local copies, waits for them, and re-layouts  1.42 us (2%)
  between operations  0.97 us (1%)
    ppermute x10, starting transfers between devices, partner_2(): lax.ppermute(value, axis, [(i, i ^ 1 << stride) for i in range(lax.axis_s...  21 us
    ppermute x10, waiting for transfers between devices, partner_2(): lax.ppermute(value, axis, [(i, i ^ 1 << stride) for i in range(lax.axis_s...  15.6 us
    dot_general x2, matrix products, matvec(): jnp.einsum('ikpq,ikq->ip', near_blocks, picked, preferred_element_type=jn...  9.15 us
    ppermute x2, starting transfers between devices, padded(): lax.ppermute(lax.slice_in_dim(block, block.shape[dim] - width, None, axis...  6.06 us
    dot_general x2, matrix products, matvec(): jnp.einsum('lrcp,cp->lcr', right_part, slip_rows, preferred_element_type=...  4.71 us
    dot_general x2, matrix products, matvec(): jnp.einsum('lrcp,lcr->cp', left_part, weights, preferred_element_type=jnp...  2.66 us
    ppermute x2, starting transfers between devices, padded(): lax.ppermute(lax.slice_in_dim(block, 0, width, axis=dim), axis, backward)  2.58 us
  transfers between devices with their start and end apart: 14, of which 10 were waited for; matrix products, arithmetic and copies ran while one was open for 13% of the time, Pallas kernels for 0%

commit v1 on v0

v1 whole, which is shorter than its diff:
```python
import functools
import math

import jax
import jax.numpy as jnp
from jax import lax
from jax.experimental import pallas as pl
from jax.experimental.pallas import tpu as pltpu
from jax.sharding import PartitionSpec as P

MESH = pl.DeviceIdType.MESH
LANES = 128
F32 = jnp.float32
BF16 = jnp.bfloat16


def flipped(me, slot):
    target = me
    bit = 1
    while bit <= slot:
        if slot & bit:
            target = target + bit * (1 - 2 * ((me // bit) % 2))
        bit *= 2
    return target


def dot_nt(a, b):
    return lax.dot_general(a, b, (((1,), (1,)), ((), ())), preferred_element_type=F32)


def dot_nn(a, b):
    return lax.dot_general(a, b, (((1,), (0,)), ((), ())), preferred_element_type=F32)


def kernel(
    n, levels, ranks_n,
    slip_ref, near_hbm, index_ref, left_hbm, right_hbm, ranks_ref,
    first_ref, second_ref,
    near_v, left_v, right_v, ext_first, ext_second, pick, dev, recv, scale_ref,
    near_sem, left_sem, right_sem, halo_send, halo_recv, far_send, far_recv,
):
    me = lax.axis_index("leaf")
    ext = (ext_first, ext_second)
    leaves, near_n, size, _ = near_v.shape
    local_levels = leaves.bit_length() - 1
    cross = levels - local_levels
    cols = levels * ranks_n
    local_cols = local_levels * ranks_n
    per_chunk = LANES // ranks_n
    right_parts = right_sem.shape[0]
    near_parts = near_sem.shape[0]
    right_width = right_v.shape[1] // right_parts
    near_width = leaves // near_parts

    barrier = pltpu.get_barrier_semaphore()
    for slot in range(1, n):
        pl.semaphore_signal(
            barrier, inc=1, device_id={"leaf": flipped(me, slot)}, device_id_type=MESH
        )

    right_copies = [
        pltpu.make_async_copy(
            right_hbm.at[:, pl.ds(part * right_width, right_width)],
            right_v.at[:, pl.ds(part * right_width, right_width)],
            right_sem.at[part],
        )
        for part in range(right_parts)
    ]
    near_copies = [
        pltpu.make_async_copy(
            near_hbm.at[pl.ds(part * near_width, near_width)],
            near_v.at[pl.ds(part * near_width, near_width)],
            near_sem.at[part],
        )
        for part in range(near_parts)
    ]
    left_copy = pltpu.make_async_copy(left_hbm, left_v, left_sem)
    for copy in right_copies:
        copy.start()
    for copy in near_copies[:1]:
        copy.start()
    left_copy.start()
    for copy in near_copies[1:]:
        copy.start()

    slip = jnp.concatenate(
        [slip_ref[pl.ds(half, leaves, stride=2), :] for half in range(2)], axis=1
    )
    dev[...] = jnp.zeros_like(dev)

    col = lax.broadcasted_iota(jnp.int32, (leaves, cols), 1)
    allowed = jnp.zeros((leaves, cols), jnp.int32)
    scale = jnp.zeros((leaves, cols), F32)
    ranks = ranks_ref[...]
    for level in range(levels):
        here = (col >= level * ranks_n) & (col < (level + 1) * ranks_n)
        allowed = jnp.where(here, ranks[:, level : level + 1] + level * ranks_n, allowed)
        scale = jnp.where(here, 1.0 / math.sqrt(size * 2**level), scale)
    scale_ref[...] = jnp.where(col < allowed, scale, 0.0)

    row_cols = lax.broadcasted_iota(jnp.int32, (leaves, cols), 0)
    row_size = lax.broadcasted_iota(jnp.int32, (leaves, size), 0)
    row_lane = lax.broadcasted_iota(jnp.int32, (leaves, LANES), 0)
    lane = lax.broadcasted_iota(jnp.int32, (leaves, LANES), 1)

    def halo_copies(call):
        own = ext[call].at[pl.ds(leaves, leaves)]
        up = pltpu.make_async_remote_copy(
            src_ref=own, dst_ref=ext[call].at[pl.ds(0, leaves)],
            send_sem=halo_send.at[call, 0], recv_sem=halo_recv.at[call, 0],
            device_id={"leaf": me + 1}, device_id_type=MESH,
        )
        down = pltpu.make_async_remote_copy(
            src_ref=own, dst_ref=ext[call].at[pl.ds(2 * leaves, leaves)],
            send_sem=halo_send.at[call, 1], recv_sem=halo_recv.at[call, 1],
            device_id={"leaf": me - 1}, device_id_type=MESH,
        )
        return up, down

    def send_halo(call):
        up, down = halo_copies(call)

        @pl.when(me < n - 1)
        def _():
            up.start()

        @pl.when(me > 0)
        def _():
            down.start()

    def receive_halo(call):
        up, down = halo_copies(call)

        @pl.when(me < n - 1)
        def _():
            up.wait_send()
            down.wait_recv()

        @pl.when(me > 0)
        def _():
            down.wait_send()
            up.wait_recv()

    def project(vector, call):
        projected = jnp.zeros((leaves, cols), F32)
        for c in range(leaves):
            if call == 0 and (c * size) % right_width == 0:
                right_copies[c * size // right_width].wait()
            part = dot_nt(vector, right_v[:, c * size : (c + 1) * size])
            projected = jnp.where(row_cols == c, part, projected)
        total = jnp.sum(projected[:, local_cols:], axis=0, keepdims=True)
        chunks = dev.shape[1]
        for chunk in range(chunks):
            width = min(LANES, total.shape[1] - chunk * LANES)
            dev[call, chunk : chunk + 1, 0:width] = total[:, chunk * LANES : chunk * LANES + width]
        return projected[:, :local_cols]

    def send_far(call):
        for slot in range(n - 1, 0, -1):
            chunk = (slot.bit_length() - 1) // per_chunk
            pltpu.make_async_remote_copy(
                src_ref=dev.at[call, pl.ds(chunk, 1)],
                dst_ref=recv.at[call, pl.ds(slot, 1)],
                send_sem=far_send.at[call], recv_sem=far_recv.at[call],
                device_id={"leaf": flipped(me, slot)}, device_id_type=MESH,
            ).start()

    def receive_far(call):
        rows = recv.at[call, pl.ds(1, n - 1)]
        pltpu.make_async_copy(rows, rows, far_send.at[call]).wait()
        pltpu.make_async_copy(rows, rows, far_recv.at[call]).wait()
        got = recv[call]
        slot = lax.broadcasted_iota(jnp.int32, (n, LANES), 0)
        slot_lane = lax.broadcasted_iota(jnp.int32, (n, LANES), 1)
        pieces = []
        for chunk in range(dev.shape[1]):
            keep = slot < 0
            for bit in range(chunk * per_chunk, min(cross, (chunk + 1) * per_chunk)):
                low = (bit - chunk * per_chunk) * ranks_n
                keep = keep | (
                    (slot >= 2**bit) & (slot < 2 ** (bit + 1))
                    & (slot_lane >= low) & (slot_lane < low + ranks_n)
                )
            piece = jnp.sum(jnp.where(keep, got, 0.0), axis=0, keepdims=True)
            width = min(LANES, cross * ranks_n - chunk * LANES)
            pieces.append(jnp.broadcast_to(piece, (leaves, LANES))[:, :width])
        sums = pieces[0] if len(pieces) == 1 else jnp.concatenate(pieces, axis=1)
        return (sums * scale_ref[:, local_cols:]).astype(BF16)

    def local_weights(projected):
        acc = projected
        sibling = jnp.zeros_like(acc)
        for level in range(local_levels):
            step = 2**level
            swapped = jnp.where(
                (row_lane // step) % 2 == 1,
                pltpu.roll(acc, step, 0),
                pltpu.roll(acc, leaves - step, 0),
            )
            here = (lane >= level * ranks_n) & (lane < (level + 1) * ranks_n)
            sibling = jnp.where(here, swapped, sibling)
            acc = acc + swapped
        return (sibling * scale_ref[:, :local_cols]).astype(BF16)

    def matvec(value, call, out_ref):
        vector = value.astype(BF16)
        ext[call][leaves : 2 * leaves, :] = vector.astype(F32)
        if call == 0:
            pl.semaphore_wait(barrier, n - 1)
        send_halo(call)
        projected = project(vector, call)
        send_far(call)
        weights = local_weights(projected)
        acc = jnp.zeros((leaves, size), F32)
        if call == 0:
            left_copy.wait()
        for c in range(leaves):
            if call == 0 and c % near_width == 0:
                near_copies[c // near_width].wait()
            part = dot_nt(vector, near_v[c, 0]) + dot_nn(
                weights, left_v[0:local_cols, c * size : (c + 1) * size]
            )
            acc = jnp.where(row_size == c, part, acc)
        receive_halo(call)
        for k in range(1, near_n):
            for c in range(leaves):
                position = jnp.clip(index_ref[k, c] - (me - 1) * leaves, 0, 3 * leaves - 1)
                pick[k - 1, c : c + 1, :] = ext[call][pl.ds(position, 1), :]
        picked = [pick[k - 1].astype(BF16) for k in range(1, near_n)]
        for c in range(leaves):
            part = dot_nt(picked[0], near_v[c, 1])
            for k in range(2, near_n):
                part = part + dot_nt(picked[k - 1], near_v[c, k])
            acc = jnp.where(row_size == c, acc + part, acc)
        weights = receive_far(call)
        for c in range(leaves):
            part = dot_nn(weights, left_v[local_cols:cols, c * size : (c + 1) * size])
            acc = jnp.where(row_size == c, acc + part, acc)
        for half in range(2):
            out_ref[pl.ds(half, leaves, stride=2), :] = acc[:, half * LANES : (half + 1) * LANES]
        return acc

    first = matvec(slip, 0, first_ref)
    relaxed = slip + jnp.tanh(first / 3.0)
    matvec(relaxed, 1, second_ref)


def local(slip_rate, near_blocks, near_index, far_left, far_right, far_ranks):
    n = lax.axis_size("leaf")
    leaves, near_n, size, _ = near_blocks.shape
    levels, ranks_n, patches = far_left.shape
    cols = levels * ranks_n
    cross = levels - (leaves.bit_length() - 1)
    chunks = -(-cross * ranks_n // LANES)
    right_parts = 4
    near_parts = 4
    shape = (patches // LANES, LANES)
    vmem = pl.BlockSpec(memory_space=pltpu.VMEM)
    anywhere = pl.BlockSpec(memory_space=pl.ANY)
    first, second = pl.pallas_call(
        functools.partial(kernel, n, levels, ranks_n),
        out_shape=[jax.ShapeDtypeStruct(shape, F32)] * 2,
        in_specs=[
            vmem, anywhere, pl.BlockSpec(memory_space=pltpu.SMEM), anywhere, anywhere, vmem,
        ],
        out_specs=[vmem, vmem],
        scratch_shapes=[
            pltpu.VMEM((leaves, near_n, size, size), BF16),
            pltpu.VMEM((cols, patches), BF16),
            pltpu.VMEM((cols, patches), BF16),
            pltpu.VMEM((3 * leaves, size), F32),
            pltpu.VMEM((3 * leaves, size), F32),
            pltpu.VMEM((near_n - 1, leaves, size), F32),
            pltpu.VMEM((2, chunks, LANES), F32),
            pltpu.VMEM((2, n, LANES), F32),
            pltpu.VMEM((leaves, cols), F32),
            pltpu.SemaphoreType.DMA((near_parts,)),
            pltpu.SemaphoreType.DMA,
            pltpu.SemaphoreType.DMA((right_parts,)),
            pltpu.SemaphoreType.DMA((2, 2)),
            pltpu.SemaphoreType.DMA((2, 2)),
            pltpu.SemaphoreType.DMA((2,)),
            pltpu.SemaphoreType.DMA((2,)),
        ],
        compiler_params=pltpu.CompilerParams(collective_id=0, has_side_effects=True),
    )(
        slip_rate.reshape(shape),
        near_blocks,
        near_index.T,
        far_left.reshape(cols, patches),
        far_right.reshape(cols, patches),
        far_ranks,
    )
    return first.reshape(-1), second.reshape(-1)


def solution(mesh):
    in_specs = (
        P(("models", "leaf")),
        P(("models", "leaf"), None, None, None),
        P(("models", "leaf"), None),
        P(None, None, ("models", "leaf")),
        P(None, None, ("models", "leaf")),
        P(("models", "leaf"), None),
    )
    out_specs = (P(("models", "leaf")), P(("models", "leaf")))
    return jax.shard_map(local, mesh=mesh, in_specs=in_specs, out_specs=out_specs, check_vma=False)
```

time: 66.2 us -> 23.6 us (0.36)
  starting transfers between devices: 29.6 us -> 0 us
  Pallas kernels: 0 us -> 19.9 us
  matrix products: 16.8 us -> 0 us
  waiting for transfers between devices: 15.6 us -> 0 us
  other arithmetic: 1.44 us -> 0 us
  local copies, waits for them, and re-layouts: 1.42 us -> 2.65 us
    ppermute x14 -> x0, starting transfers between devices: 29.6 us -> none  [the longest x10 21 us: partner_2(): lax.ppermute(value, axis, [(i, i ^ 1 << stride) for i in range(lax.axis_s...]
    pallas_call x0 -> x1, Pallas kernels: none -> 19.9 us  [local(): pl.pallas_call(functools.partial(kernel, n, levels, ranks_n), out_shape=[...]
    dot_general x8 -> x0, matrix products: 16.8 us -> none  [the longest x2 9.15 us: matvec(): jnp.einsum('ikpq,ikq->ip', near_blocks, picked, preferred_element_type=jn...]
    ppermute x14 -> x0, waiting for transfers between devices: 15.6 us -> none  [the longest x10 15.6 us: partner_2(): lax.ppermute(value, axis, [(i, i ^ 1 << stride) for i in range(lax.axis_s...]
    unnamed x32 -> x2, local copies, waits for them, and re-layouts: 0.9 us -> 2.65 us
    convert_element_type x4 -> x0, other arithmetic: 1.05 us -> none  [the longest x1 0.87 us: local(): slip_bf = slip_rate.astype(jnp.bfloat16)]
  transfers between devices with their start and end apart: 14 -> 0, of which waited for: 10 -> 0; matrix products, arithmetic and copies ran while one was open for 13% -> 0% of each run, Pallas kernels for 0% -> 0%
where the time goes in v1:
time: 23.6 us; the launch traced here: 23.2 us
  Pallas kernels  19.9 us (84%)
  local copies, waits for them, and re-layouts  2.65 us (11%)
  between operations  0.64 us (3%)
    pallas_call x1, Pallas kernels, local(): pl.pallas_call(functools.partial(kernel, n, levels, ranks_n), out_shape=[...  19.9 us
    unnamed x2, local copies, waits for them, and re-layouts  2.65 us

profile of v1, /device:TPU:0, one launch (start us, length us, event | category | flops | bytes accessed | tf_op | source)
XLA Modules:
  0.0 23.2 jit_solution(2168964007399759599)
XLA Ops:
  0.6 19.9 %shard_map.77 = (f32[32,128]{1,0:T(8,128)}, f32[32,128]{1,0:T(8,128)}) custom-call(f32[32,128]{1,0:T(8,128)} %bitcast.8, bf16[16,3,256,256]{3,2,1,0:T(8,128)(2,1)} %near_hbm.1, s32[3,16]{1,0:T(4,128)} %bitcast.11, bf16[288,4096]{1,0:T(8,128)(2,1)} %bitcast.6, bf16[288,4096]{1,0:T(8,128)(2,1)} %bitcast.7, s32[16,9]{1,0:T(8,128)} %ranks_ref.1), custom_call_target="tpu_custom_call" | custom-call | tf_op jit(solution)/shard_map/pallas_call | solution.py:260
  20.5 1.3 %copy.10 = f32[4096]{0:T(1024)} copy(f32[4096]{0:T(1024)} %bitcast.10) | data formatting | bytes 32768
  21.9 1.3 %copy.11 = f32[4096]{0:T(1024)} copy(f32[4096]{0:T(1024)} %bitcast.9) | data formatting | bytes 32768
